TPU v7x, 256 devices: a whole 4x4x8 slice. The times are simulated.
256 devices in a mesh: seq: 32 (over y, z), head: 8 (over x, core).
Axes of the slice: x: 4, y: 4, z: 8, core: 2. Of those that a mesh axis runs over, the one named last changes fastest.
Arguments:
- tokens: bfloat16 [2, 4096, 2560], P(None, 'seq', 'head'), may hold values from -6 to 6
- token_mix: float32 [5, 2560], replicated, may hold values from 0.05 to 0.95
- receptance: bfloat16 [2560, 2560], P(None, 'head'), may hold values from -0.125 to 0.125
- key_weight: bfloat16 [2560, 2560], P(None, 'head'), may hold values from -0.125 to 0.125
- value_weight: bfloat16 [2560, 2560], P(None, 'head'), may hold values from -0.125 to 0.125
- decay_base: float32 [2560], P('head'), may hold values from -12.5 to -1.9
- decay_down_matrix: bfloat16 [2560, 96], replicated, may hold values from -0.125 to 0.125
- decay_up_matrix: bfloat16 [96, 2560], P(None, 'head'), may hold values from -0.625 to 0.625
- learn_base: float32 [2560], P('head'), may hold values from -1.5 to 1.5
- learning_down_matrix: bfloat16 [2560, 96], replicated, may hold values from -0.125 to 0.125
- learning_up_matrix: bfloat16 [96, 2560], P(None, 'head'), may hold values from -0.625 to 0.625
- key_scale: float32 [2560], P('head'), may hold values from 0.25 to 1.75
- key_blend: float32 [2560], P('head'), may hold values from 0.2 to 1
- norm_gain: float32 [2560], P('head'), may hold values from 0.25 to 1.75
- norm_bias: float32 [2560], P('head'), may hold values from -3 to 3
- output_weight: bfloat16 [2560, 2560], P('head'), may hold values from -0.125 to 0.125
Outputs:
- mixed_out: bfloat16 [2, 4096, 2560], P(None, 'seq', 'head')
All inputs are finite; a program needn't handle non-finite values.
Results may differ from a plain program's by a relative error of at most 0.014.
Values may be sent and summed in bfloat16 or wider, within the bound.
No kernel may reach another device: no remote copies, remote signals or barrier semaphores. Data moves between devices by JAX's collectives and lax.ppermute only.
A program may use at most 128 MiB of HBM per device.

v0:
```python
import jax
import jax.numpy as jnp
from jax import lax
from jax.sharding import Mesh
from jax.sharding import PartitionSpec as P

HEAD_SIZE = 64
SPAN = 64
SEQ = ("seq_0", "seq_1")


def shifted(block, axis, distance):
    devices = range(lax.axis_size(axis))
    route = [(i - distance, i) for i in devices if i - distance in devices]
    return lax.ppermute(block, axis, route)


def gather_turned(arrays, axis, dims):
    turned = [jnp.moveaxis(a, dim, 0) for a, dim in zip(arrays, dims)]
    widths = [t[0].size for t in turned]
    both = jnp.concatenate([t.reshape(-1, w) for t, w in zip(turned, widths)], axis=1)
    out = lax.all_gather(both, axis, axis=0, tiled=True)
    tiles = jnp.split(out, [sum(widths[:k]) for k in range(1, len(widths))], axis=1)
    return tuple(
        (
            jnp.moveaxis(b.reshape(-1, *t.shape[1:]), 0, dim)
            for b, t, dim in zip(tiles, turned, dims)
        )
    )


def filled_with(value, identity):
    return jnp.broadcast_to(jnp.asarray(identity, value.dtype), value.shape)


def prefix_by_axis(value, axes, combine, identity):
    before = start = filled_with(value, identity)
    running = value
    for axis in reversed(axes):
        length, position = (lax.axis_size(axis), lax.axis_index(axis))
        pieces = lax.all_gather(running, axis)
        inside, running = (start, start)
        for k in range(length):
            passed = k < position
            running = combine(running, pieces[k])
            inside = jnp.where(passed, running, inside)
        before = combine(inside, before)
    return before


def joined_along(tiles, dim):
    dims = list(tiles.shape[1:])
    dims[dim] *= tiles.shape[0]
    return jnp.moveaxis(tiles, 0, dim).reshape(dims)


def from_everyone(value, axis):
    copies = jnp.broadcast_to(value, (lax.axis_size(axis), *value.shape))
    return lax.all_to_all(copies, axis, split_axis=0, concat_axis=0, tiled=True)


def gather_directly(value, axis, dim):
    return joined_along(from_everyone(value, axis), dim)


def matmul(left, right):
    return jnp.matmul(left, right)


def combine_maps(earlier, later):
    size = later.shape[-2]
    moving = later[..., size:]
    adding = later[..., :size]
    return matmul(moving, earlier) + jnp.concatenate([adding, jnp.zeros_like(adding)], axis=-1)


def lower_pairs(first, second, keep):
    products = jnp.einsum("abcti,abcsi->abcts", first, second)
    return jnp.where(keep, products, 0.0)


def body(
    tokens,
    token_mix,
    receptance,
    key_weight,
    value_weight,
    decay_base,
    decay_down_matrix,
    decay_up_matrix,
    learn_base,
    learning_down_matrix,
    learning_up_matrix,
    key_scale,
    key_blend,
    norm_gain,
    norm_bias,
    output_weight,
):
    seq_count, length, local_width = tokens.shape
    row_count = seq_count * length
    head_count = local_width // HEAD_SIZE
    boundary = shifted(tokens[:, length - 1 :, :], SEQ, 1)
    weights = (receptance, decay_down_matrix, key_weight, value_weight, learning_down_matrix)
    feature_piece, edge_piece = gather_turned((tokens, boundary), "head", (2, 2))
    extent = feature_piece.shape[2]
    current = feature_piece.astype(jnp.float32)
    earlier = jnp.concatenate([edge_piece, feature_piece[:, :-1, :]], axis=1).astype(jnp.float32)
    change = earlier - current
    result = []
    for term_index in range(5):
        blended = (
            (current + change * token_mix[term_index])
            .astype(jnp.bfloat16)
            .reshape(row_count, extent)
        )
        weight_rows = weights[term_index]
        result.append(jnp.dot(blended, weight_rows, preferred_element_type=jnp.float32))
    recept_out, decay_pre, key_raw, value_out, learn_pre = tuple(result)
    decay_hidden = jnp.tanh(decay_pre).astype(jnp.bfloat16)
    learn_hidden = learn_pre.astype(jnp.bfloat16)
    decay_arg = decay_base + jnp.dot(
        decay_hidden, decay_up_matrix, preferred_element_type=jnp.float32
    )
    log_decay = -jnp.exp(-jax.nn.softplus(-decay_arg) - 0.5)
    learn_rate = jax.nn.sigmoid(
        learn_base + jnp.dot(learn_hidden, learning_up_matrix, preferred_element_type=jnp.float32)
    )
    scaled = (key_raw * key_scale).reshape(row_count, head_count, HEAD_SIZE)
    unit_key = (
        scaled / jnp.sqrt(jnp.sum(scaled * scaled, axis=-1, keepdims=True) + 1e-06)
    ).reshape(row_count, local_width)
    key_final = key_raw * (1.0 + (learn_rate - 1.0) * key_blend)
    span_count = length // SPAN

    def arrange(values):
        return values.reshape(seq_count, span_count, SPAN, head_count, HEAD_SIZE).transpose(
            0, 3, 1, 2, 4
        )

    recept_c = arrange(recept_out)
    decay_c = arrange(log_decay)
    unit_c = arrange(unit_key)
    learn_c = arrange(learn_rate)
    key_c = arrange(key_final)
    value_c = arrange(value_out)
    alpha_c = -unit_c
    beta_c = unit_c * learn_c
    cumul = jnp.cumsum(decay_c, axis=3)
    before_c = cumul - decay_c
    middle = cumul[:, :, :, SPAN // 2 - 1 : SPAN // 2, :]
    ending = cumul[:, :, :, SPAN - 1 :, :]
    left_alpha = alpha_c * jnp.exp(before_c - middle)
    left_recept = recept_c * jnp.exp(cumul - middle)
    right_beta = beta_c * jnp.exp(middle - cumul)
    right_key = key_c * jnp.exp(middle - cumul)
    positions = jnp.arange(SPAN)
    strict = positions[:, None] > positions[None, :]
    within = positions[:, None] >= positions[None, :]
    lower_ab = lower_pairs(left_alpha, right_beta, strict)
    lower_ak = lower_pairs(left_alpha, right_key, strict)
    lower_rb = lower_pairs(left_recept, right_beta, within)
    lower_rk = lower_pairs(left_recept, right_key, within)
    identity = jnp.eye(SPAN, dtype=jnp.float32)
    inverse = identity + lower_ab
    power = lower_ab
    for level in range(SPAN.bit_length() - 2):
        power = matmul(power, power)
        inverse = inverse + matmul(power, inverse)
    gain_key = matmul(inverse, alpha_c * jnp.exp(before_c))
    gain_value = matmul(inverse, matmul(lower_ak, value_c))
    query_eff = recept_c * jnp.exp(cumul) + matmul(lower_rb, gain_key)
    local_out = matmul(lower_rb, gain_value) + matmul(lower_rk, value_c)
    beta_end = beta_c * jnp.exp(ending - cumul)
    key_end = key_c * jnp.exp(ending - cumul)
    head_eye = jnp.eye(HEAD_SIZE, dtype=jnp.float32)
    transition = jnp.einsum("abctj,abctk->abcjk", beta_end, gain_key)
    transition = transition + head_eye * jnp.swapaxes(jnp.exp(ending), -1, -2)
    increment = jnp.einsum("abctk,abctv->abckv", beta_end, gain_value)
    increment = increment + jnp.einsum("abctk,abctv->abckv", key_end, value_c)
    start_aug = jnp.broadcast_to(
        jnp.concatenate([jnp.zeros((HEAD_SIZE, HEAD_SIZE), jnp.float32), head_eye], axis=1),
        (seq_count, head_count, HEAD_SIZE, 2 * HEAD_SIZE),
    )

    def advance(carry, step_items):
        moving, adding = step_items
        following = matmul(moving, carry) + jnp.concatenate(
            [adding, jnp.zeros_like(adding)], axis=-1
        )
        return (following, carry)

    total, entries = lax.scan(
        advance, start_aug, (jnp.moveaxis(transition, 2, 0), jnp.moveaxis(increment, 2, 0))
    )
    prefix = prefix_by_axis(total, SEQ, combine_maps, start_aug)
    state_in = prefix[..., :HEAD_SIZE]
    span_state = entries[..., :HEAD_SIZE] + matmul(entries[..., HEAD_SIZE:], state_in)
    span_state = jnp.moveaxis(span_state, 0, 2)
    output_c = matmul(query_eff, span_state) + local_out
    wkv = output_c.transpose(0, 2, 3, 1, 4).reshape(row_count, head_count, HEAD_SIZE)
    centred = wkv - jnp.mean(wkv, axis=-1, keepdims=True)
    spread = jnp.mean(centred * centred, axis=-1, keepdims=True)
    normed = (centred / jnp.sqrt(spread + 0.00064)).reshape(
        row_count, local_width
    ) * norm_gain + norm_bias
    normed = normed.astype(jnp.bfloat16)
    own_columns = lax.all_to_all(output_weight, "head", split_axis=1, concat_axis=0, tiled=True)
    weight_rows = own_columns
    result = jnp.dot(
        gather_directly(normed, "head", 1), weight_rows, preferred_element_type=jnp.float32
    )
    return result.astype(jnp.bfloat16).reshape(seq_count, length, local_width)


def solution(mesh):
    torus = Mesh(mesh.devices.reshape(4, 8, mesh.shape["head"]), ("seq_0", "seq_1", "head"))
    placed = (
        P(None, SEQ, "head"),
        P(),
        P(None, "head"),
        P(None, "head"),
        P(None, "head"),
        P("head"),
        P(),
        P(None, "head"),
        P("head"),
        P(),
        P(None, "head"),
        P("head"),
        P("head"),
        P("head"),
        P("head"),
        P("head", None),
    )
    return jax.shard_map(
        body, mesh=torus, in_specs=placed, out_specs=P(None, SEQ, "head"), check_vma=False
    )
```

profile of v0, /device:TPU:1, one launch (start us, length us, event | category | flops | bytes accessed | tf_op | source)
XLA Modules:
  0.0 227.0 jit_solution(18370085318308386240)
XLA Ops:
  6.5 1.2 slice.141
  7.7 4.4 %collective-permute-start = (bf16[2,1,320]{1,2,0:T(8,128)(2,1)S(1)}, bf16[2,1,320]{1,2,0:T(8,128)(2,1)S(1)}, u32[]{:S(2)}, u32[]{:S(2)}) collective-permute-start(bf16[2,1,320]{1,2,0:T(8,128)(2,1)S(1)} %slice.141), channel_id=1, source_target_pairs={{0,8},{8,16},{16,24},{24,32},{32,40},{40,48},{48,56},{56,64},{64,7... | collective-permute-start | bytes 3848 | tf_op jit(solution)/shard_map/ppermute | solution.py:15
  12.1 0.9 copy_bitcast_fusion
  13.0 1.9 collective-permute-done
  14.9 2.0 copy.177
  17.0 0.8 copy.124
  18.1 32.8 %all-gather.11.cloned.1.call-done = bf16[8,320,258]{1,2,0:T(8,128)(2,1)} async-done(((bf16[1,320,258]{1,2,0:T(8,128)(2,1)}), bf16[8,320,258]{1,2,0:T(8,128)(2,1)}) %all-gather.11.cloned.1.call-update) | async-done | bytes 1320976 | tf_op jit(solution)/shard_map/all_gather | solution.py:22
  50.9 1.6 copy.125
  52.5 2.4 %reshape.160 = bf16[2560,258]{0,1:T(8,128)(2,1)} reshape(bf16[8,320,258]{1,0,2:T(8,128)(2,1)S(1)} %copy.125) | data formatting | bytes 2641920
  54.9 1.4 split.8
  56.3 0.8 slice_bitcast_fusion
  57.2 3.4 %fusion.3 = (bf16[2,128,2560]{2,1,0:T(8,128)(2,1)}, bf16[2,128,2560]{2,1,0:T(8,128)(2,1)S(1)}, bf16[2,128,2560]{2,1,0:T(8,128)(2,1)}, bf16[2,128,2560]{2,1,0:T(8,128)(2,1)}, bf16[2,128,2560]{2,1,0:T(8,128)(2,1)}) fusion(bf16[2,128,2560]{2,1,0:T(8,128)(2,1)S(1)} %bitcast.218, f32[2560]{0:T(1024)S(1)} %get-tuple-element.55, ...), kind=kLoop, calls=%fused_computation.12 | loop fusion | flops 13762560 | bytes 9226240 | tf_op jit(solution)/shard_map/convert_element_type | solution.py:114
  60.5 2.0 fusion.75
  62.9 1.3 copy.178
  64.2 1.3 copy.127
  65.5 2.3 %fusion.32 = f32[256,320]{0,1:T(8,128)S(1)} fusion(bf16[96,320]{1,0:T(8,128)(2,1)S(1)} %copy-done.39, bf16[256,2560]{1,0:T(8,128)(2,1)} %bitcast.226, bf16[2560,96]{0,1:T(8,128)(2,1)} %param.27, f32[320]{0:T(512)S(1)} %copy-done.41), kind=kOutput, calls=%fused_computation.66 | convolution fusion | flops 141910016 | bytes 2192640 | tf_op jit(solution)/shard_map/dot_general | solution.py:127
  67.9 1.2 reshape.129
  69.1 3.0 %fusion.134 = (f32[256,320]{0,1:T(8,128)S(1)}, f32[256,320]{0,1:T(8,128)}, f32[256,320]{0,1:T(8,128)}) fusion(f32[320]{0:T(512)S(1)} %copy-done.34, f32[320]{0:T(512)S(1)} %copy-done.35, f32[256,320]{0,1:T(8,128)} %copy-done.9, bf16[256,2560]{1,0:T(8,128)(2,1)S(1)} %bitcast.221, bf16[2560,320]{0,1:T(8,128)(2,1)} %param.21), kind=kOutput, calls=%fused_computation.205 | convolution fusion | flops 419921920 | bytes 4262400 | tf_op jit(solution)/shard_map/dot_general | solution.py:118
  72.1 1.4 reshape.127
  73.5 1.3 copy.133
  75.2 1.3 copy.147
  76.7 1.7 reduce_window_sum.11
  78.4 1.3 copy.134
  79.7 4.9 %bitcast_multiply_fusion = (bf16[2,5,2,64,64]{4,3,1,2,0:T(8,128)(2,1)}, bf16[2,5,2,64,64]{4,3,1,2,0:T(8,128)(2,1)S(1)}, bf16[2,5,2,64,64]{4,3,1,2,0:T(8,128)(2,1...) fusion(f32[2,2,64,5,64]{4,2,3,1,0:T(8,128)} %copy.147, ...), kind=kOutput, calls=%fused_computation.78 | convolution fusion | flops 421232640 | bytes 6077440 | tf_op jit(solution)/shard_map/dot_general | solution.py:118
  85.6 1.1 convolution_select_fusion.1
  88.2 3.1 %convolution_bitcast_fusion.2 = bf16[2,5,2,64,64]{4,3,1,2,0:T(8,128)(2,1)S(1)} fusion(bf16[2,2,64,2560,1]{3,2,4,1,0:T(8,128)(2,1)} %bitcast.224, bf16[5,64,2560,1,1]{2,1,0,4,3:T(8,128)(2,1)} %bitcast.235), kind=kOutput, calls=%fused_computation.39 | convolution fusion | flops 419430400 | bytes 3112960 | tf_op jit(solution)/shard_map/dot_general | solution.py:118
  91.6 1.5 fusion.17
  93.4 1.3 fusion.16
  94.6 1.1 fusion.13
  95.8 2.4 %while.12 = (s32[]{:T(128)}, f32[2,5,64,128]{3,2,1,0:T(8,128)S(1)}, f32[2,2,5,64,128]{4,3,2,1,0:T(8,128)}, bf16[2,2,5,64,64]{4,3,0,2,1:T(8,128)(2,1)}, f32[2,2,5,64,64]{4,3,0,2,1:T(8,128)S(1)}, /*index=5*/s32[]{:T(128)}) while((s32[]{:T(128)}, f32[2,5,64,128]{3,2,1,0:T(8,128)S(1)}, f32[2,2,5,64,128]{4,3,2,1,0:T(8,128)}, ...), condition=%wide.region_3.4_spmd, body=%wide.region_2.3_spmd.sunk | while | flops 10567682 | bytes 3441257 | solution.py:193
  95.8 0.8 bitcast_dynamic-update-slice_fusion.2
  97.0 0.8 bitcast_dynamic-update-slice_fusion.2
  98.2 0.7 copy-done.1
  99.2 38.7 %all-gather.7.cloned.1.call-done = f32[16,5,64,128]{3,2,1,0:T(8,128)} async-done(((f32[2,5,64,128]{3,2,1,0:T(8,128)}), f32[16,5,64,128]{3,2,1,0:T(8,128)}) %all-gather.7.cloned.1.call-update) | async-done | bytes 2621456 | tf_op jit(solution)/shard_map/all_gather | solution.py:41
  137.9 1.3 convolution_add_fusion.21
  139.2 0.7 copy-done.30
  139.8 1.3 convolution_add_fusion.20
  141.2 1.3 convolution_add_fusion.19
  142.5 0.7 copy-done.14
  143.2 1.3 convolution_add_fusion.18
  144.5 0.7 copy-done.16
  145.2 1.3 convolution_add_fusion.17
  146.5 0.7 copy-done.18
  147.2 1.3 convolution_add_fusion.16
  148.5 0.6 copy-done.20
  149.1 1.3 convolution_add_fusion.15
  150.5 0.7 copy-done.22
  151.1 2.0 convolution_add_fusion.14
  153.2 3.8 %copy.165 = bf16[320,2560]{0,1:T(8,128)(2,1)} copy(bf16[320,2560]{1,0:T(8,128)(2,1)} %param.33) | data formatting | bytes 3276800 | tf_op args[15]
  157.0 8.1 %all-to-all-start.1 = ((bf16[320,8,320]{0,2,1:T(8,128)(2,1)}), bf16[320,8,320]{0,2,1:T(8,128)(2,1)}, u32[]{:S(2)}, u32[]{:S(2)}) async-start(bf16[320,8,320]{0,2,1:T(8,128)(2,1)} %bitcast.220), calls=%async_computation.1 | async-start | bytes 3932160 | tf_op jit(solution)/shard_map/all_to_all | solution.py:208
  165.2 1.5 convolution_select_fusion.3
  166.7 1.2 fusion.144
  167.9 2.0 convolution_add_fusion.8
  170.3 11.1 %all-gather.9.cloned.1.call-done = f32[8,5,64,128]{3,2,1,0:T(8,128)} async-done(((f32[2,5,64,128]{3,2,1,0:T(8,128)}), f32[8,5,64,128]{3,2,1,0:T(8,128)}) %all-gather.9.cloned.1.call-update) | async-done | bytes 1310736 | tf_op jit(solution)/shard_map/all_gather | solution.py:41
  181.3 1.3 convolution_add_fusion.12
  182.6 1.3 convolution_add_fusion.11
  184.0 1.3 convolution_add_fusion.10
  185.3 2.2 fusion.28
  187.6 1.8 fusion.12
  189.4 1.2 fusion.45
  190.6 1.8 fusion.135
  194.1 23.6 %all_to_all.21 = bf16[8,256,320]{1,2,0:T(8,128)(2,1)S(1)} all-to-all(bf16[8,256,320]{1,2,0:T(8,128)(2,1)S(1)} %broadcast_in_dim.60), channel_id=1, replica_groups=mesh['seq_0'=4,'seq_1'=8,'head'=8] {'head'}, dimensions={0} | all-to-all | bytes 2621440 | tf_op jit(solution)/shard_map/all_to_all | solution.py:59
  217.7 2.1 fusion.39
  219.8 0.7 copy.248
  (136 shorter events, 7.5 us)
Async XLA Ops:
  6.5 73.2 %copy-start = (bf16[2560,320]{0,1:T(8,128)(2,1)S(1)}, bf16[2560,320]{0,1:T(8,128)(2,1)}, u32[]{:S(2)}) copy-start(bf16[2560,320]{0,1:T(8,128)(2,1)} %param.20) | copy-start | bytes 4915204
  6.5 11.5 %copy-start.33 = (f32[5,2560]{1,0:T(8,128)S(1)}, f32[5,2560]{1,0:T(8,128)}, u32[]{:S(2)}) copy-start(f32[5,2560]{1,0:T(8,128)} %param.19) | copy-start | bytes 153604
  6.5 44.4 %all-gather.11.cloned.1.call-start = ((), (), s32[]{:S(2)}) async-start(), calls=%async_computation.4 | async-start | bytes 1824768 | tf_op jit(solution)/shard_map/all_gather | solution.py:22
  7.7 7.2 %collective-permute-start = (bf16[2,1,320]{1,2,0:T(8,128)(2,1)S(1)}, bf16[2,1,320]{1,2,0:T(8,128)(2,1)S(1)}, u32[]{:S(2)}, u32[]{:S(2)}) collective-permute-start(bf16[2,1,320]{1,2,0:T(8,128)(2,1)S(1)} %slice.141), channel_id=1, source_target_pairs={{0,8},{8,16},{16,24},{24,32},{32,40},{40,48},{48,56},{56,64},{64,7... | collective-permute-start | bytes 3848 | tf_op jit(solution)/shard_map/ppermute | solution.py:15
  17.8 120.0 %all-gather.7.cloned.1.call-start = ((), (), s32[]{:S(2)}) async-start(), calls=%async_computation.2 | async-start | bytes 2949120 | tf_op jit(solution)/shard_map/all_gather | solution.py:41
  57.1 3.4 %copy-start.38 = (bf16[96,320]{1,0:T(8,128)(2,1)S(1)}, bf16[96,320]{1,0:T(8,128)(2,1)}, u32[]{:S(2)}) copy-start(bf16[96,320]{1,0:T(8,128)(2,1)} %param.25) | copy-start | bytes 184324
  57.1 3.4 %copy-start.40 = (f32[320]{0:T(512)S(1)}, f32[320]{0:T(512)}, u32[]{:S(2)}) copy-start(f32[320]{0:T(512)} %param.23) | copy-start | bytes 3844
  62.5 3.0 %copy-start.39 = (bf16[96,320]{1,0:T(8,128)(2,1)S(1)}, bf16[96,320]{1,0:T(8,128)(2,1)}, u32[]{:S(2)}) copy-start(bf16[96,320]{1,0:T(8,128)(2,1)} %param.28) | copy-start | bytes 184324
  62.5 3.0 %copy-start.41 = (f32[320]{0:T(512)S(1)}, f32[320]{0:T(512)}, u32[]{:S(2)}) copy-start(f32[320]{0:T(512)} %param.26) | copy-start | bytes 3844
  65.5 3.6 %copy-start.2 = (bf16[2,128,2560]{2,1,0:T(8,128)(2,1)S(1)}, bf16[2,128,2560]{2,1,0:T(8,128)(2,1)}, u32[]{:S(2)}) copy-start(bf16[2,128,2560]{2,1,0:T(8,128)(2,1)} %get-tuple-element.74) | copy-start | bytes 3932164
  65.5 3.6 %copy-start.34 = (f32[320]{0:T(512)S(1)}, f32[320]{0:T(512)}, u32[]{:S(2)}) copy-start(f32[320]{0:T(512)} %param.29) | copy-start | bytes 3844
  65.5 3.6 %copy-start.35 = (f32[320]{0:T(512)S(1)}, f32[320]{0:T(512)}, u32[]{:S(2)}) copy-start(f32[320]{0:T(512)} %param.30) | copy-start | bytes 3844
  67.9 1.2 copy-start.9
  72.1 2.7 %copy-start.8 = (f32[256,320]{0,1:T(8,128)S(1)}, f32[256,320]{0,1:T(8,128)}, u32[]{:S(2)}) copy-start(f32[256,320]{0,1:T(8,128)} %get-tuple-element.93) | copy-start | bytes 983044
  75.2 3.2 %copy-start.6 = (f32[2,2,64,5,64]{2,1,0,4,3:T(2,128)S(1)}, f32[2,2,64,5,64]{2,1,0,4,3:T(2,128)}, u32[]{:S(2)}) copy-start(f32[2,2,64,5,64]{2,1,0,4,3:T(2,128)} %reshape.129) | copy-start | bytes 983044
  78.3 6.2 %copy-start.3 = (f32[2,5,2,64,64]{4,3,2,1,0:T(8,128)}, f32[2,5,2,64,64]{4,3,2,1,0:T(8,128)S(1)}, u32[]{:S(2)}) copy-start(f32[2,5,2,64,64]{4,3,2,1,0:T(8,128)S(1)} %reduce_window_sum.11) | copy-start | bytes 983044
  84.6 0.8 copy-start.25
  84.6 1.0 copy-start.24
  88.2 3.1 %copy-start.28 = (bf16[2,5,2,64,64]{4,3,1,2,0:T(8,128)(2,1)S(1)}, bf16[2,5,2,64,64]{4,3,1,2,0:T(8,128)(2,1)}, u32[]{:S(2)}) copy-start(bf16[2,5,2,64,64]{4,3,1,2,0:T(8,128)(2,1)} %get-tuple-element.88) | copy-start | bytes 491524
  91.3 1.7 copy-start.26
  91.6 3.1 %copy-start.11 = (bf16[2,5,2,64,64]{4,3,2,1,0:T(8,128)(2,1)}, bf16[2,5,2,64,64]{4,3,2,1,0:T(8,128)(2,1)S(1)}, u32[]{:S(2)}) copy-start(bf16[2,5,2,64,64]{4,3,2,1,0:T(8,128)(2,1)S(1)} %fusion.51) | copy-start | bytes 491524
  93.1 1.6 copy-start.27
  95.8 42.1 %copy-start.32 = (pred[128]{0:T(512)(128)(4,1)S(1)}, pred[128]{0:T(512)(128)(4,1)}, u32[]{:S(2)}) copy-start(pred[128]{0:T(512)(128)(4,1)} %constant.67.clone.1) | copy-start | bytes 388
  95.8 1.0 copy-start.7
  97.0 1.0 copy-start.7
  98.2 0.7 copy-start.1
  98.9 82.4 %all-gather.9.cloned.1.call-start = ((), (), s32[]{:S(2)}) async-start(), calls=%async_computation.3 | async-start | bytes 1638400 | tf_op jit(solution)/shard_map/all_gather | solution.py:41
  139.2 0.7 copy-start.30
  142.5 0.7 copy-start.14
  144.5 0.7 copy-start.16
  146.5 0.7 copy-start.18
  148.5 0.7 copy-start.20
  150.5 0.7 copy-start.22
  157.0 37.0 %all-to-all-start.1 = ((bf16[320,8,320]{0,2,1:T(8,128)(2,1)}), bf16[320,8,320]{0,2,1:T(8,128)(2,1)}, u32[]{:S(2)}, u32[]{:S(2)}) async-start(bf16[320,8,320]{0,2,1:T(8,128)(2,1)} %bitcast.220), calls=%async_computation.1 | async-start | bytes 3932160 | tf_op jit(solution)/shard_map/all_to_all | solution.py:208
  165.1 2.8 %copy-start.4 = (f32[2,5,2,64,64]{4,3,2,1,0:T(8,128)S(1)}, f32[2,5,2,64,64]{4,3,2,1,0:T(8,128)}, u32[]{:S(2)}) copy-start(f32[2,5,2,64,64]{4,3,2,1,0:T(8,128)} %copy-done.3) | copy-start | bytes 983044
  165.1 2.8 %copy-start.13 = (f32[2,5,2,64,64]{4,3,1,2,0:T(8,128)S(1)}, f32[2,5,2,64,64]{4,3,1,2,0:T(8,128)}, u32[]{:S(2)}) copy-start(f32[2,5,2,64,64]{4,3,1,2,0:T(8,128)} %get-tuple-element.94) | copy-start | bytes 983044
  166.6 3.2 %copy-start.12 = (f32[2,5,64,128]{3,2,1,0:T(8,128)S(1)}, f32[2,5,64,128]{3,2,1,0:T(8,128)}, u32[]{:S(2)}) copy-start(f32[2,5,64,128]{3,2,1,0:T(8,128)} %convolution_add_fusion.14) | copy-start | bytes 983044
  166.7 3.2 %copy-start.15 = (bf16[2,5,64,128]{3,2,1,0:T(8,128)(2,1)S(1)}, bf16[2,5,64,128]{3,2,1,0:T(8,128)(2,1)}, u32[]{:S(2)}) copy-start(bf16[2,5,64,128]{3,2,1,0:T(8,128)(2,1)} %copy-done.14) | copy-start | bytes 491524
  166.7 3.2 %copy-start.17 = (bf16[2,5,64,128]{3,2,1,0:T(8,128)(2,1)S(1)}, bf16[2,5,64,128]{3,2,1,0:T(8,128)(2,1)}, u32[]{:S(2)}) copy-start(bf16[2,5,64,128]{3,2,1,0:T(8,128)(2,1)} %copy-done.16) | copy-start | bytes 491524
  166.7 3.2 %copy-start.19 = (bf16[2,5,64,128]{3,2,1,0:T(8,128)(2,1)S(1)}, bf16[2,5,64,128]{3,2,1,0:T(8,128)(2,1)}, u32[]{:S(2)}) copy-start(bf16[2,5,64,128]{3,2,1,0:T(8,128)(2,1)} %copy-done.18) | copy-start | bytes 491524
  166.7 3.2 %copy-start.21 = (bf16[2,5,64,128]{3,2,1,0:T(8,128)(2,1)S(1)}, bf16[2,5,64,128]{3,2,1,0:T(8,128)(2,1)}, u32[]{:S(2)}) copy-start(bf16[2,5,64,128]{3,2,1,0:T(8,128)(2,1)} %copy-done.20) | copy-start | bytes 491524
  166.7 3.2 %copy-start.23 = (bf16[2,5,64,128]{3,2,1,0:T(8,128)(2,1)S(1)}, bf16[2,5,64,128]{3,2,1,0:T(8,128)(2,1)}, u32[]{:S(2)}) copy-start(bf16[2,5,64,128]{3,2,1,0:T(8,128)(2,1)} %copy-done.22) | copy-start | bytes 491524
  166.7 3.2 %copy-start.31 = (bf16[2,5,64,128]{3,2,1,0:T(8,128)(2,1)S(1)}, bf16[2,5,64,128]{3,2,1,0:T(8,128)(2,1)}, u32[]{:S(2)}) copy-start(bf16[2,5,64,128]{3,2,1,0:T(8,128)(2,1)} %copy-done.30) | copy-start | bytes 491524
  170.2 15.1 %copy-start.29 = (f32[2,5,64,128]{3,2,1,0:T(8,128)}, f32[2,5,64,128]{3,2,1,0:T(8,128)S(1)}, u32[]{:S(2)}) copy-start(f32[2,5,64,128]{3,2,1,0:T(8,128)S(1)} %convolution_add_fusion.13) | copy-start | bytes 983044
  185.3 4.1 %copy-start.10 = (bf16[2,5,2,64,64]{4,3,1,2,0:T(8,128)(2,1)S(1)}, bf16[2,5,2,64,64]{4,3,1,2,0:T(8,128)(2,1)}, u32[]{:S(2)}) copy-start(bf16[2,5,2,64,64]{4,3,1,2,0:T(8,128)(2,1)} %convolution_add_fusion.8) | copy-start | bytes 491524
  187.6 3.1 %copy-start.5 = (f32[2,5,2,64,64]{3,4,2,1,0:T(8,128)S(1)}, f32[2,5,2,64,64]{3,4,2,1,0:T(8,128)}, u32[]{:S(2)}) copy-start(f32[2,5,2,64,64]{3,4,2,1,0:T(8,128)} %fusion.144) | copy-start | bytes 983044
  192.4 1.4 copy-start.36
  192.4 1.4 copy-start.37
Sparse Core Ops, SparseCore 0:
  17.9 32.9 all-gather.10
  99.0 38.7 all-gather.6
  153.3 27.9 all-gather.8
where the time goes:
time: 228 us; the launch traced here: 227 us
  waiting for transfers between devices  84.5 us (37%)
  matrix products  52.8 us (23%)
  local copies, waits for them, and re-layouts  34 us (15%)
  blocking collectives  23.6 us (10%)
  between operations  13.9 us (6%)
  starting transfers between devices  12.8 us (6%)
  other arithmetic  5.44 us (2%)
    all_gather x2, waiting for transfers between devices, prefix_by_axis(): pieces = lax.all_gather(running, axis)  49.7 us
    all_gather x1, waiting for transfers between devices, gather_turned(): out = lax.all_gather(both, axis, axis=0, tiled=True)  32.8 us
    dot_general x31, matrix products, matmul(): return jnp.matmul(left, right)  30 us
    all_to_all x1, blocking collectives, from_everyone(): return lax.all_to_all(copies, axis, split_axis=0, concat_axis=0, tiled=True)  23.6 us
    unnamed x84, local copies, waits for them, and re-layouts  11 us
    dot_general x3, matrix products, body(): jnp.dot(blended, weight_rows, preferred_element_type=jnp.float32)  10.9 us
    all_to_all x1, starting transfers between devices, body(): lax.all_to_all(output_weight, 'head', split_axis=1, concat_axis=0, tiled=...  8.09 us
    reshape x6, local copies, waits for them, and re-layouts, arrange(): values.reshape(seq_count, span_count, SPAN, head_count, HEAD_SIZE)  5.87 us
  transfers between devices with their start and end apart: 5, of which 4 were waited for; matrix products, arithmetic and copies ran while one was open for 10% of the time, Pallas kernels for 0%

commit v1 on v0

--- a/solution.py
+++ b/solution.py
@@ -19,7 +19,8 @@
     turned = [jnp.moveaxis(a, dim, 0) for a, dim in zip(arrays, dims)]
     widths = [t[0].size for t in turned]
     both = jnp.concatenate([t.reshape(-1, w) for t, w in zip(turned, widths)], axis=1)
-    out = lax.all_gather(both, axis, axis=0, tiled=True)
+    stack = jnp.stack([both] * lax.axis_size(axis))
+    out = jnp.concatenate(lax.all_to_all(stack, axis, 0, 0), axis=0)
     tiles = jnp.split(out, [sum(widths[:k]) for k in range(1, len(widths))], axis=1)
     return tuple(
         (

time: 228 us -> 221 us (0.969)
  waiting for transfers between devices: 84.5 us -> 77.7 us
  starting transfers between devices: 12.8 us -> 18.5 us
  local copies, waits for them, and re-layouts: 34 us -> 29.4 us
    all_gather x1 -> x0, waiting for transfers between devices: 32.8 us -> none  [gather_turned(): out = lax.all_gather(both, axis, axis=0, tiled=True)]
    all_to_all x0 -> x1, waiting for transfers between devices: none -> 20.9 us  [gather_turned(): out = jnp.concatenate(lax.all_to_all(stack, axis, 0, 0), axis=0)]
    all_to_all x0 -> x1, starting transfers between devices: none -> 5.96 us  [gather_turned(): out = jnp.concatenate(lax.all_to_all(stack, axis, 0, 0), axis=0)]
    unnamed x84 -> x85, local copies, waits for them, and re-layouts: 11 us -> 5.37 us
    all_gather x2, waiting for transfers between devices: 49.7 us -> 54.9 us  [prefix_by_axis(): pieces = lax.all_gather(running, axis)]
    reshape x0 -> x1, local copies, waits for them, and re-layouts: none -> 2.78 us  [gather_turned(): out = jnp.concatenate(lax.all_to_all(stack, axis, 0, 0), axis=0)]
  transfers between devices with their start and end apart: 5 -> 5, of which waited for: 4 -> 4; matrix products, arithmetic and copies ran while one was open for 10% -> 9% of each run, Pallas kernels for 0% -> 0%
where the time goes in v1:
time: 221 us; the launch traced here: 220 us
  waiting for transfers between devices  77.7 us (35%)
  matrix products  51.1 us (23%)
  local copies, waits for them, and re-layouts  29.4 us (13%)
  blocking collectives  23.6 us (11%)
  starting transfers between devices  18.5 us (8%)
  between operations  14.3 us (6%)
  other arithmetic  5.26 us (2%)
    all_gather x2, waiting for transfers between devices, prefix_by_axis(): pieces = lax.all_gather(running, axis)  54.9 us
    dot_general x31, matrix products, matmul(): return jnp.matmul(left, right)  28.2 us
    all_to_all x1, blocking collectives, from_everyone(): return lax.all_to_all(copies, axis, split_axis=0, concat_axis=0, tiled=True)  23.6 us
    all_to_all x1, waiting for transfers between devices, gather_turned(): out = jnp.concatenate(lax.all_to_all(stack, axis, 0, 0), axis=0)  20.9 us
    dot_general x3, matrix products, body(): jnp.dot(blended, weight_rows, preferred_element_type=jnp.float32)  10.9 us
    all_to_all x1, starting transfers between devices, body(): lax.all_to_all(output_weight, 'head', split_axis=1, concat_axis=0, tiled=...  8.11 us
    all_to_all x1, starting transfers between devices, gather_turned(): out = jnp.concatenate(lax.all_to_all(stack, axis, 0, 0), axis=0)  5.96 us
    reshape x6, local copies, waits for them, and re-layouts, arrange(): values.reshape(seq_count, span_count, SPAN, head_count, HEAD_SIZE)  5.87 us
  transfers between devices with their start and end apart: 5, of which 4 were waited for; matrix products, arithmetic and copies ran while one was open for 9% of the time, Pallas kernels for 0%

profile of v1, /device:TPU:1, one launch (start us, length us, event | category | flops | bytes accessed | tf_op | source)
XLA Modules:
  0.0 219.9 jit_solution(7857282521917453723)
XLA Ops:
  6.5 1.1 slice.141
  7.7 4.4 %collective-permute-start = (bf16[2,1,320]{1,2,0:T(8,128)(2,1)S(1)}, bf16[2,1,320]{1,2,0:T(8,128)(2,1)S(1)}, u32[]{:S(2)}, u32[]{:S(2)}) collective-permute-start(bf16[2,1,320]{1,2,0:T(8,128)(2,1)S(1)} %slice.141), channel_id=1, source_target_pairs={{0,8},{8,16},{16,24},{24,32},{32,40},{40,48},{48,56},{56,64},{64,7... | collective-permute-start | bytes 3848 | tf_op jit(solution)/shard_map/ppermute | solution.py:15
  12.1 0.9 copy_bitcast_fusion
  13.0 1.9 collective-permute-done
  14.9 2.0 copy.177
  17.1 1.3 stack.2
  18.5 6.0 %all-to-all-start = ((bf16[8,320,258]{1,2,0:T(8,128)(2,1)}), bf16[8,320,258]{1,2,0:T(8,128)(2,1)S(1)}, u32[]{:S(2)}, u32[]{:S(2)}) async-start(bf16[8,320,258]{1,2,0:T(8,128)(2,1)} %stack.2), calls=%async_computation | async-start | bytes 3244032 | tf_op jit(solution)/shard_map/all_to_all | solution.py:23
  24.7 20.9 %all-to-all-done = bf16[8,320,258]{1,2,0:T(8,128)(2,1)S(1)} async-done(((bf16[8,320,258]{1,2,0:T(8,128)(2,1)}), bf16[8,320,258]{1,2,0:T(8,128)(2,1)S(1)}, u32[]{:S(2)}, u32[]{:S(2)}) %all-to-all-start) | async-done | bytes 1320992 | tf_op jit(solution)/shard_map/all_to_all | solution.py:23
  45.5 1.4 copy.125
  46.9 2.8 %reshape.127 = bf16[2560,258]{0,1:T(8,128)(2,1)S(1)} reshape(bf16[8,320,258]{1,0,2:T(8,128)(2,1)} %copy.125) | data formatting | bytes 2641920 | tf_op jit(solution)/shard_map/reshape | solution.py:23
  49.9 3.2 %fusion.3 = (bf16[2,128,2560]{2,1,0:T(8,128)(2,1)}, bf16[2,128,2560]{2,1,0:T(8,128)(2,1)S(1)}, bf16[2,128,2560]{2,1,0:T(8,128)(2,1)}, bf16[2,128,2560]{2,1,0:T(8,128)(2,1)}, bf16[2,128,2560]{2,1,0:T(8,128)(2,1)}) fusion(bf16[2,128,2560]{2,1,0:T(8,128)(2,1)S(1)} %bitcast.217, f32[2560]{0:T(1024)S(1)} %get-tuple-element.55, ...), kind=kLoop, calls=%fused_computation.12 | loop fusion | flops 13762560 | bytes 9226240 | tf_op jit(solution)/shard_map/convert_element_type | solution.py:115
  53.1 2.0 fusion.75
  55.1 0.4 reshape.131
  55.5 1.3 copy.178
  56.8 1.3 copy.127
  58.0 2.3 %fusion.32 = f32[256,320]{0,1:T(8,128)S(1)} fusion(bf16[96,320]{1,0:T(8,128)(2,1)S(1)} %copy-done.40, bf16[256,2560]{1,0:T(8,128)(2,1)} %bitcast.225, bf16[2560,96]{0,1:T(8,128)(2,1)} %param.27, f32[320]{0:T(512)S(1)} %copy-done.42), kind=kOutput, calls=%fused_computation.66 | convolution fusion | flops 141910016 | bytes 2192640 | tf_op jit(solution)/shard_map/dot_general | solution.py:128
  60.4 1.2 reshape.135
  61.6 3.0 %fusion.134 = (f32[256,320]{0,1:T(8,128)S(1)}, f32[256,320]{0,1:T(8,128)}, f32[256,320]{0,1:T(8,128)}) fusion(f32[320]{0:T(512)S(1)} %copy-done.35, f32[320]{0:T(512)S(1)} %copy-done.36, f32[256,320]{0,1:T(8,128)} %copy-done.9, bf16[256,2560]{1,0:T(8,128)(2,1)S(1)} %bitcast.220, bf16[2560,320]{0,1:T(8,128)(2,1)} %param.21), kind=kOutput, calls=%fused_computation.205 | convolution fusion | flops 419921920 | bytes 4262400 | tf_op jit(solution)/shard_map/dot_general | solution.py:119
  64.6 1.4 reshape.133
  66.0 1.3 copy.133
  67.3 0.4 reshape.136
  67.7 1.3 copy.147
  69.2 1.7 reduce_window_sum.11
  70.9 1.3 copy.134
  72.2 4.9 %bitcast_multiply_fusion = (bf16[2,5,2,64,64]{4,3,1,2,0:T(8,128)(2,1)}, bf16[2,5,2,64,64]{4,3,1,2,0:T(8,128)(2,1)S(1)}, bf16[2,5,2,64,64]{4,3,1,2,0:T(8,128)(2,1...) fusion(f32[2,2,64,5,64]{4,2,3,1,0:T(8,128)} %copy.147, ...), kind=kOutput, calls=%fused_computation.78 | convolution fusion | flops 421232640 | bytes 6077440 | tf_op jit(solution)/shard_map/dot_general | solution.py:119
  78.1 1.1 convolution_select_fusion.1
  80.4 0.4 convolution_add_fusion.1
  80.8 3.1 %convolution_bitcast_fusion.2 = bf16[2,5,2,64,64]{4,3,1,2,0:T(8,128)(2,1)S(1)} fusion(bf16[2,2,64,2560,1]{3,2,4,1,0:T(8,128)(2,1)} %bitcast.223, bf16[5,64,2560,1,1]{2,1,0,4,3:T(8,128)(2,1)} %bitcast.233), kind=kOutput, calls=%fused_computation.39 | convolution fusion | flops 419430400 | bytes 3112960 | tf_op jit(solution)/shard_map/dot_general | solution.py:119
  83.9 1.0 fusion.51
  84.9 0.4 fusion.17
  85.6 1.3 fusion.16
  86.9 1.1 fusion.13
  88.0 2.4 %while.12 = (s32[]{:T(128)}, f32[2,5,64,128]{3,2,1,0:T(8,128)S(1)}, f32[2,2,5,64,128]{4,3,2,1,0:T(8,128)}, bf16[2,2,5,64,64]{4,3,0,2,1:T(8,128)(2,1)}, f32[2,2,5,64,64]{4,3,0,2,1:T(8,128)S(1)}, /*index=5*/s32[]{:T(128)}) while((s32[]{:T(128)}, f32[2,5,64,128]{3,2,1,0:T(8,128)S(1)}, f32[2,2,5,64,128]{4,3,2,1,0:T(8,128)}, ...), condition=%wide.region_3.4_spmd, body=%wide.region_2.3_spmd.sunk | while | flops 10567682 | bytes 3441257 | solution.py:194
  88.1 0.8 bitcast_dynamic-update-slice_fusion.2
  89.2 0.8 bitcast_dynamic-update-slice_fusion.2
  90.4 0.7 copy-done.1
  91.2 42.2 %all-gather.5.cloned.1.call-done = f32[16,5,64,128]{3,2,1,0:T(8,128)} async-done(((f32[2,5,64,128]{3,2,1,0:T(8,128)}), f32[16,5,64,128]{3,2,1,0:T(8,128)}) %all-gather.5.cloned.1.call-update) | async-done | bytes 2621456 | tf_op jit(solution)/shard_map/all_gather | solution.py:42
  133.4 1.3 convolution_add_fusion.21
  134.8 0.7 copy-done.31
  135.4 1.3 convolution_add_fusion.20
  136.7 1.3 convolution_add_fusion.19
  138.1 1.4 convolution_add_fusion.18
  139.5 1.4 convolution_add_fusion.17
  140.9 1.4 convolution_add_fusion.16
  142.3 1.4 convolution_add_fusion.15
  143.7 2.1 convolution_add_fusion.14
  145.8 3.8 %copy.165 = bf16[320,2560]{0,1:T(8,128)(2,1)} copy(bf16[320,2560]{1,0:T(8,128)(2,1)} %param.33) | data formatting | bytes 3276800 | tf_op args[15]
  149.7 8.1 %all-to-all-start.2 = ((bf16[320,8,320]{0,2,1:T(8,128)(2,1)}), bf16[320,8,320]{0,2,1:T(8,128)(2,1)}, u32[]{:S(2)}, u32[]{:S(2)}) async-start(bf16[320,8,320]{0,2,1:T(8,128)(2,1)} %bitcast.219), calls=%async_computation.2 | async-start | bytes 3932160 | tf_op jit(solution)/shard_map/all_to_all | solution.py:209
  157.8 1.5 convolution_select_fusion.3
  159.4 1.2 fusion.144
  160.9 0.3 convolution_add_fusion.13
  161.2 12.7 %all-gather.7.cloned.1.call-done = f32[8,5,64,128]{3,2,1,0:T(8,128)} async-done(((f32[2,5,64,128]{3,2,1,0:T(8,128)}), f32[8,5,64,128]{3,2,1,0:T(8,128)}) %all-gather.7.cloned.1.call-update) | async-done | bytes 1310736 | tf_op jit(solution)/shard_map/all_gather | solution.py:42
  173.9 1.3 convolution_add_fusion.12
  175.2 1.3 convolution_add_fusion.11
  176.6 1.3 convolution_add_fusion.10
  177.9 2.2 fusion.28
  180.1 1.8 fusion.12
  182.0 1.2 fusion.45
  183.1 1.8 fusion.135
  185.0 0.5 copy.162
  185.7 0.6 reshape.137
  186.7 23.6 %all_to_all.26 = bf16[8,256,320]{1,2,0:T(8,128)(2,1)S(1)} all-to-all(bf16[8,256,320]{1,2,0:T(8,128)(2,1)S(1)} %broadcast_in_dim.60), channel_id=1, replica_groups=mesh['seq_0'=4,'seq_1'=8,'head'=8] {'head'}, dimensions={0} | all-to-all | bytes 2621440 | tf_op jit(solution)/shard_map/all_to_all | solution.py:60
  210.2 2.1 fusion.39
  212.4 0.7 copy.248
  (138 shorter events, 5.0 us)
Async XLA Ops:
  6.5 65.7 %copy-start = (bf16[2560,320]{0,1:T(8,128)(2,1)S(1)}, bf16[2560,320]{0,1:T(8,128)(2,1)}, u32[]{:S(2)}) copy-start(bf16[2560,320]{0,1:T(8,128)(2,1)} %param.20) | copy-start | bytes 4915204
  7.7 7.2 %collective-permute-start = (bf16[2,1,320]{1,2,0:T(8,128)(2,1)S(1)}, bf16[2,1,320]{1,2,0:T(8,128)(2,1)S(1)}, u32[]{:S(2)}, u32[]{:S(2)}) collective-permute-start(bf16[2,1,320]{1,2,0:T(8,128)(2,1)S(1)} %slice.141), channel_id=1, source_target_pairs={{0,8},{8,16},{16,24},{24,32},{32,40},{40,48},{48,56},{56,64},{64,7... | collective-permute-start | bytes 3848 | tf_op jit(solution)/shard_map/ppermute | solution.py:15
  18.5 6.1 %copy-start.34 = (f32[5,2560]{1,0:T(8,128)S(1)}, f32[5,2560]{1,0:T(8,128)}, u32[]{:S(2)}) copy-start(f32[5,2560]{1,0:T(8,128)} %param.19) | copy-start | bytes 153604
  18.5 27.1 %all-to-all-start = ((bf16[8,320,258]{1,2,0:T(8,128)(2,1)}), bf16[8,320,258]{1,2,0:T(8,128)(2,1)S(1)}, u32[]{:S(2)}, u32[]{:S(2)}) async-start(bf16[8,320,258]{1,2,0:T(8,128)(2,1)} %stack.2), calls=%async_computation | async-start | bytes 3244032 | tf_op jit(solution)/shard_map/all_to_all | solution.py:23
  24.4 109.0 %all-gather.5.cloned.1.call-start = ((), (), s32[]{:S(2)}) async-start(), calls=%async_computation.3 | async-start | bytes 2949120 | tf_op jit(solution)/shard_map/all_gather | solution.py:42
  49.8 3.2 %copy-start.39 = (bf16[96,320]{1,0:T(8,128)(2,1)S(1)}, bf16[96,320]{1,0:T(8,128)(2,1)}, u32[]{:S(2)}) copy-start(bf16[96,320]{1,0:T(8,128)(2,1)} %param.25) | copy-start | bytes 184324
  49.9 3.2 %copy-start.41 = (f32[320]{0:T(512)S(1)}, f32[320]{0:T(512)}, u32[]{:S(2)}) copy-start(f32[320]{0:T(512)} %param.23) | copy-start | bytes 3844
  55.1 3.0 %copy-start.40 = (bf16[96,320]{1,0:T(8,128)(2,1)S(1)}, bf16[96,320]{1,0:T(8,128)(2,1)}, u32[]{:S(2)}) copy-start(bf16[96,320]{1,0:T(8,128)(2,1)} %param.28) | copy-start | bytes 184324
  55.1 3.0 %copy-start.42 = (f32[320]{0:T(512)S(1)}, f32[320]{0:T(512)}, u32[]{:S(2)}) copy-start(f32[320]{0:T(512)} %param.26) | copy-start | bytes 3844
  58.0 3.6 %copy-start.2 = (bf16[2,128,2560]{2,1,0:T(8,128)(2,1)S(1)}, bf16[2,128,2560]{2,1,0:T(8,128)(2,1)}, u32[]{:S(2)}) copy-start(bf16[2,128,2560]{2,1,0:T(8,128)(2,1)} %get-tuple-element.74) | copy-start | bytes 3932164
  58.0 3.6 %copy-start.35 = (f32[320]{0:T(512)S(1)}, f32[320]{0:T(512)}, u32[]{:S(2)}) copy-start(f32[320]{0:T(512)} %param.29) | copy-start | bytes 3844
  58.0 3.6 %copy-start.36 = (f32[320]{0:T(512)S(1)}, f32[320]{0:T(512)}, u32[]{:S(2)}) copy-start(f32[320]{0:T(512)} %param.30) | copy-start | bytes 3844
  60.4 1.2 copy-start.9
  64.6 2.7 %copy-start.8 = (f32[256,320]{0,1:T(8,128)S(1)}, f32[256,320]{0,1:T(8,128)}, u32[]{:S(2)}) copy-start(f32[256,320]{0,1:T(8,128)} %get-tuple-element.93) | copy-start | bytes 983044
  67.7 3.2 %copy-start.6 = (f32[2,2,64,5,64]{2,1,0,4,3:T(2,128)S(1)}, f32[2,2,64,5,64]{2,1,0,4,3:T(2,128)}, u32[]{:S(2)}) copy-start(f32[2,2,64,5,64]{2,1,0,4,3:T(2,128)} %reshape.135) | copy-start | bytes 983044
  70.9 6.2 %copy-start.3 = (f32[2,5,2,64,64]{4,3,2,1,0:T(8,128)}, f32[2,5,2,64,64]{4,3,2,1,0:T(8,128)S(1)}, u32[]{:S(2)}) copy-start(f32[2,5,2,64,64]{4,3,2,1,0:T(8,128)S(1)} %reduce_window_sum.11) | copy-start | bytes 983044
  77.1 0.8 copy-start.25
  77.1 1.0 copy-start.24
  80.7 3.1 %copy-start.29 = (bf16[2,5,2,64,64]{4,3,1,2,0:T(8,128)(2,1)S(1)}, bf16[2,5,2,64,64]{4,3,1,2,0:T(8,128)(2,1)}, u32[]{:S(2)}) copy-start(bf16[2,5,2,64,64]{4,3,1,2,0:T(8,128)(2,1)} %get-tuple-element.88) | copy-start | bytes 491524
  80.8 4.1 %copy-start.28 = (bf16[2,5,2,64,64]{4,3,2,1,0:T(8,128)(2,1)S(1)}, bf16[2,5,2,64,64]{4,3,2,1,0:T(8,128)(2,1)}, u32[]{:S(2)}) copy-start(bf16[2,5,2,64,64]{4,3,2,1,0:T(8,128)(2,1)} %convolution_select_fusion.1) | copy-start | bytes 491524
  83.9 1.4 copy-start.26
  85.3 1.6 copy-start.10
  85.3 1.6 copy-start.27
  88.0 45.4 %copy-start.33 = (pred[128]{0:T(512)(128)(4,1)S(1)}, pred[128]{0:T(512)(128)(4,1)}, u32[]{:S(2)}) copy-start(pred[128]{0:T(512)(128)(4,1)} %constant.67.clone.1) | copy-start | bytes 388
  88.0 1.0 copy-start.7
  89.2 1.0 copy-start.7
  90.4 0.7 copy-start.1
  91.1 82.8 %all-gather.7.cloned.1.call-start = ((), (), s32[]{:S(2)}) async-start(), calls=%async_computation.4 | async-start | bytes 1638400 | tf_op jit(solution)/shard_map/all_gather | solution.py:42
  134.8 0.7 copy-start.31
  138.1 7.7 %copy-start.14 = (bf16[2,5,64,128]{3,2,1,0:T(8,128)(2,1)}, bf16[2,5,64,128]{3,2,1,0:T(8,128)(2,1)S(1)}, u32[]{:S(2)}) copy-start(bf16[2,5,64,128]{3,2,1,0:T(8,128)(2,1)S(1)} %convolution_add_fusion.19) | copy-start | bytes 491524
  139.5 10.2 %copy-start.16 = (bf16[2,5,64,128]{3,2,1,0:T(8,128)(2,1)}, bf16[2,5,64,128]{3,2,1,0:T(8,128)(2,1)S(1)}, u32[]{:S(2)}) copy-start(bf16[2,5,64,128]{3,2,1,0:T(8,128)(2,1)S(1)} %convolution_add_fusion.18) | copy-start | bytes 491524
  140.9 8.8 %copy-start.18 = (bf16[2,5,64,128]{3,2,1,0:T(8,128)(2,1)}, bf16[2,5,64,128]{3,2,1,0:T(8,128)(2,1)S(1)}, u32[]{:S(2)}) copy-start(bf16[2,5,64,128]{3,2,1,0:T(8,128)(2,1)S(1)} %convolution_add_fusion.17) | copy-start | bytes 491524
  142.3 7.4 %copy-start.20 = (bf16[2,5,64,128]{3,2,1,0:T(8,128)(2,1)}, bf16[2,5,64,128]{3,2,1,0:T(8,128)(2,1)S(1)}, u32[]{:S(2)}) copy-start(bf16[2,5,64,128]{3,2,1,0:T(8,128)(2,1)S(1)} %convolution_add_fusion.16) | copy-start | bytes 491524
  143.7 6.0 %copy-start.22 = (bf16[2,5,64,128]{3,2,1,0:T(8,128)(2,1)}, bf16[2,5,64,128]{3,2,1,0:T(8,128)(2,1)S(1)}, u32[]{:S(2)}) copy-start(bf16[2,5,64,128]{3,2,1,0:T(8,128)(2,1)S(1)} %convolution_add_fusion.15) | copy-start | bytes 491524
  149.7 36.9 %all-to-all-start.2 = ((bf16[320,8,320]{0,2,1:T(8,128)(2,1)}), bf16[320,8,320]{0,2,1:T(8,128)(2,1)}, u32[]{:S(2)}, u32[]{:S(2)}) async-start(bf16[320,8,320]{0,2,1:T(8,128)(2,1)} %bitcast.219), calls=%async_computation.2 | async-start | bytes 3932160 | tf_op jit(solution)/shard_map/all_to_all | solution.py:209
  157.8 2.8 %copy-start.4 = (f32[2,5,2,64,64]{4,3,2,1,0:T(8,128)S(1)}, f32[2,5,2,64,64]{4,3,2,1,0:T(8,128)}, u32[]{:S(2)}) copy-start(f32[2,5,2,64,64]{4,3,2,1,0:T(8,128)} %copy-done.3) | copy-start | bytes 983044
  157.8 2.8 %copy-start.11 = (bf16[2,5,2,64,64]{4,3,2,1,0:T(8,128)(2,1)S(1)}, bf16[2,5,2,64,64]{4,3,2,1,0:T(8,128)(2,1)}, u32[]{:S(2)}) copy-start(bf16[2,5,2,64,64]{4,3,2,1,0:T(8,128)(2,1)} %fusion.51) | copy-start | bytes 491524
  157.8 2.8 %copy-start.13 = (f32[2,5,2,64,64]{4,3,1,2,0:T(8,128)S(1)}, f32[2,5,2,64,64]{4,3,1,2,0:T(8,128)}, u32[]{:S(2)}) copy-start(f32[2,5,2,64,64]{4,3,1,2,0:T(8,128)} %get-tuple-element.94) | copy-start | bytes 983044
  159.3 1.5 copy-start.12
  159.3 1.5 copy-start.15
  159.3 1.5 copy-start.17
  159.3 1.5 copy-start.19
  159.4 1.5 copy-start.21
  159.4 1.5 copy-start.23
  159.4 1.5 copy-start.32
  161.2 16.7 %copy-start.30 = (f32[2,5,64,128]{3,2,1,0:T(8,128)}, f32[2,5,64,128]{3,2,1,0:T(8,128)S(1)}, u32[]{:S(2)}) copy-start(f32[2,5,64,128]{3,2,1,0:T(8,128)S(1)} %convolution_add_fusion.13) | copy-start | bytes 983044
  180.1 3.0 %copy-start.5 = (f32[2,5,2,64,64]{3,4,2,1,0:T(8,128)S(1)}, f32[2,5,2,64,64]{3,4,2,1,0:T(8,128)}, u32[]{:S(2)}) copy-start(f32[2,5,2,64,64]{3,4,2,1,0:T(8,128)} %fusion.144) | copy-start | bytes 983044
  184.9 1.4 copy-start.37
  184.9 1.4 copy-start.38
Sparse Core Ops, SparseCore 0:
  91.3 42.1 all-gather.4
  145.9 27.9 all-gather.6
